TPU v7x, 32 devices: a whole 2x2x4 slice. The times are simulated.
32 devices in a mesh: heads: 4 (over y, core), tokens: 4 (over z), cols: 2 (over x).
Axes of the slice: x: 2, y: 2, z: 4, core: 2. Of those that a mesh axis runs over, the one named last changes fastest.
Arguments:
- query_in: bfloat16 [2048, 8192], P('tokens', ('heads', 'cols')), may hold values from -24 to 24
- key_in: bfloat16 [2048, 8192], P('tokens', ('heads', 'cols')), may hold values from -24 to 24
- value_in: bfloat16 [2048, 8192], P('tokens', ('heads', 'cols')), may hold values from -6 to 6
- out_grads: bfloat16 [2048, 8192], P('tokens', ('heads', 'cols')), may hold values from -6 to 6
- doc_starts: int32 [6], replicated, may hold values from 0 to 2047, as said below
Outputs:
- input_factor: float32 [8192, 8192], P('heads', ('tokens', 'cols'))
- grad_factor: float32 [8192, 8192], P('heads', ('tokens', 'cols'))
Inputs may be any that keep to these rules, and one draw needn't show every extreme that they name: Strictly increasing with the first entry 0; document d runs from doc_starts[d] to the next start (the last one to 2048) - 1. One document holds (4 // 2 + 1) * 512 tokens.
All inputs are finite; a program needn't handle non-finite values.
Results may differ from a plain program's by a relative error of at most 0.0041.
Values may be sent and summed in bfloat16 or wider, within the bound.
A program may use at most 128 MiB of HBM per device.

v0:
```python
import math
import jax
import jax.numpy as jnp
from jax import lax
from jax.sharding import PartitionSpec as P

HEAD_DIM = 128
MASK_FLOOR = -1e30


def spread(value, axis, source):
    kept = jnp.where(lax.axis_index(axis) == source, value, 0).astype(value.dtype)
    return lax.psum(kept, axis)


def document_ids(positions, doc_starts):
    return jnp.sum((positions[:, None] >= doc_starts[None, :]).astype(jnp.int32), axis=1) - 1


def pair_scores(query_rows, key_rows, query_pos, key_pos, doc_starts):
    head_count = query_rows.shape[1] // HEAD_DIM
    query_heads = query_rows.reshape(query_rows.shape[0], head_count, HEAD_DIM)
    key_heads = key_rows.reshape(key_rows.shape[0], head_count, HEAD_DIM)
    scores = jnp.einsum(
        "qhd,khd->hqk", query_heads, key_heads, preferred_element_type=jnp.float32
    ) * (1.0 / math.sqrt(HEAD_DIM))
    query_docs = document_ids(query_pos, doc_starts)
    key_docs = document_ids(key_pos, doc_starts)
    allowed = query_docs[:, None] == key_docs[None, :]
    return (scores, allowed[None, :, :])


def on_device(query_in, key_in, value_in, out_grads, doc_starts):
    tok_dev, row_width = query_in.shape
    head_count = row_width // HEAD_DIM
    first_pos = lax.axis_index("tokens") * tok_dev
    query_pos = first_pos + jnp.arange(tok_dev, dtype=jnp.int32)
    keys_all, values_all = (
        lax.all_gather(key_in, "tokens", axis=0, tiled=True),
        lax.all_gather(value_in, "tokens", axis=0, tiled=True),
    )
    all_tokens = keys_all.shape[0]
    key_span = min(512, all_tokens)
    block_ids = jnp.arange(all_tokens // key_span, dtype=jnp.int32)

    def block_scores(block_id):
        key_begin = block_id * key_span
        key_rows = lax.dynamic_slice_in_dim(keys_all, key_begin, key_span, 0)
        key_pos = key_begin + jnp.arange(key_span, dtype=jnp.int32)
        scores, allowed = pair_scores(query_in, key_rows, query_pos, key_pos, doc_starts)
        return (key_begin, scores, allowed)

    def gated(block_id, update, running):
        key_begin = block_id * key_span
        return update(running)

    def stats_step(running, block_id):

        def update(state):
            row_peak, row_mass = state
            key_begin, scores, allowed = block_scores(block_id)
            masked = jnp.where(allowed, scores, MASK_FLOOR)
            new_peak = jnp.maximum(row_peak, jnp.max(masked, axis=2))
            new_mass = row_mass * jnp.exp(row_peak - new_peak) + jnp.sum(
                jnp.where(allowed, jnp.exp(masked - new_peak[:, :, None]), 0.0), axis=2
            )
            return (new_peak, new_mass)

        return (gated(block_id, update, running), None)

    initial = (
        jnp.full((head_count, tok_dev), MASK_FLOOR, jnp.float32),
        jnp.zeros((head_count, tok_dev), jnp.float32),
    )
    (row_peak, row_mass), _ = lax.scan(stats_step, initial, block_ids)
    log_total = row_peak + jnp.log(row_mass)

    def value_step(running, block_id):

        def update(state):
            weighted, partials = state
            key_begin, scores, allowed = block_scores(block_id)
            weights = jnp.where(allowed, jnp.exp(scores - log_total[:, :, None]), 0.0).astype(
                jnp.bfloat16
            )
            value_rows = lax.dynamic_slice_in_dim(values_all, key_begin, key_span, 0).reshape(
                key_span, head_count, HEAD_DIM
            )
            weighted = weighted + jnp.einsum(
                "hqk,khd->qhd", weights, value_rows, preferred_element_type=jnp.float32
            )
            return (weighted, partials)

        return (gated(block_id, update, running), None)

    partial_rows = 8
    value_init = (
        jnp.zeros((tok_dev, head_count, HEAD_DIM), jnp.float32),
        jnp.zeros((partial_rows, row_width), jnp.float32),
    )
    (weighted, partials), _ = lax.scan(value_step, value_init, block_ids)
    attended = weighted.reshape(tok_dev, row_width).astype(jnp.bfloat16)
    stats_all = lax.all_gather(log_total.T, "tokens", axis=0, tiled=True)
    query_rows = lax.all_gather(query_in, "tokens", axis=0, tiled=True)
    grad_rows = lax.all_gather(out_grads, "tokens", axis=0, tiled=True)
    piece_rows = query_rows.shape[0]
    piece_pos = jnp.arange(piece_rows, dtype=jnp.int32)

    def update(grad_sum):
        scores, allowed = pair_scores(query_rows, key_in, piece_pos, query_pos, doc_starts)
        weights = jnp.where(allowed, jnp.exp(scores - stats_all.T[:, :, None]), 0.0).astype(
            jnp.bfloat16
        )
        piece_grads = grad_rows.reshape(piece_rows, head_count, HEAD_DIM)
        return jnp.einsum("hqk,qhd->khd", weights, piece_grads, preferred_element_type=jnp.float32)

    summed = update(jnp.zeros((tok_dev, head_count, HEAD_DIM), jnp.float32))
    value_grads = summed.reshape(tok_dev, row_width).astype(jnp.bfloat16)
    token_shards = lax.axis_size("tokens")
    col_shards = lax.axis_size("cols")
    rows_attended, rows_grads = (
        lax.all_gather(attended[None], ("tokens", "cols"), axis=0, tiled=True),
        lax.all_gather(value_grads[None], ("tokens", "cols"), axis=0, tiled=True),
    )
    rows_attended = rows_attended.reshape(token_shards, col_shards, tok_dev, row_width)
    rows_grads = rows_grads.reshape(token_shards, col_shards, tok_dev, row_width)
    own_attended = lax.dynamic_index_in_dim(
        rows_attended, lax.axis_index("cols"), 1, keepdims=False
    )
    own_grads = lax.dynamic_index_in_dim(rows_grads, lax.axis_index("cols"), 1, keepdims=False)
    cols_attended, cols_grads = (
        spread(own_attended, "heads", lax.axis_index("tokens")),
        spread(own_grads, "heads", lax.axis_index("tokens")),
    )
    input_factor = jnp.einsum(
        "acnf,ang->cfg", rows_attended, cols_attended, preferred_element_type=jnp.float32
    )
    grad_factor = jnp.einsum(
        "acnf,ang->cfg", rows_grads, cols_grads, preferred_element_type=jnp.float32
    )
    input_factor = input_factor.reshape(col_shards * row_width, row_width) / all_tokens
    grad_factor = grad_factor.reshape(col_shards * row_width, row_width) / all_tokens
    return (input_factor, grad_factor)


def solution(mesh):
    in_specs = (
        P("tokens", ("heads", "cols")),
        P("tokens", ("heads", "cols")),
        P("tokens", ("heads", "cols")),
        P("tokens", ("heads", "cols")),
        P(),
    )
    out_specs = (P("heads", ("tokens", "cols")), P("heads", ("tokens", "cols")))
    return jax.shard_map(
        on_device, mesh=mesh, in_specs=in_specs, out_specs=out_specs, check_vma=False
    )
```

profile of v0, /device:TPU:0, one launch (start us, length us, event | category | flops | bytes accessed | tf_op | source)
XLA Modules:
  0.0 775.8 jit_solution(3249628128545039161)
XLA Ops:
  7.2 2.4 copy.58
  9.7 2.3 copy.57
  15.1 78.1 %all-gather.9.cloned.1.call-done = bf16[2048,1024]{0,1:T(8,128)(2,1)} async-done(((bf16[512,1024]{0,1:T(8,128)(2,1)}), bf16[2048,1024]{0,1:T(8,128)(2,1)}) %all-gather.9.cloned.1.call-update) | async-done | bytes 4194320 | tf_op jit(solution)/shard_map/all_gather | solution.py:39
  93.2 27.0 %while.30 = (s32[]{:T(128)}, f32[8,512]{1,0:T(8,128)S(1)}, f32[8,512]{1,0:T(8,128)S(1)}, s32[6]{0:T(128)S(1)}, s32[4]{0:T(128)S(1)}, /*index=5*/bf16[2048,1024]{...) while((s32[]{:T(128)}, f32[8,512]{1,0:T(8,128)S(1)}, ...), condition=%wide.region_5.6_spmd.clone, body=%wide.region_0.5_spmd.clone.sunk | while | flops 553950208 | bytes 21995748 | solution.py:75
  120.3 54.3 %all-gather.7.cloned.1.call-done = bf16[2048,1024]{0,1:T(8,128)(2,1)} async-done(((bf16[512,1024]{0,1:T(8,128)(2,1)}), bf16[2048,1024]{0,1:T(8,128)(2,1)}) %all-gather.7.cloned.1.call-update) | async-done | bytes 4194320 | tf_op jit(solution)/shard_map/all_gather | solution.py:40
  174.6 34.2 %while.31 = (s32[]{:T(128)}, f32[512,8,128]{0,2,1:T(8,128)}, s32[4]{0:T(128)S(1)}, bf16[2048,1024]{0,1:T(8,128)(2,1)}, s32[6]{0:T(128)S(1)}, /*index=5*/bf16[204...) while((s32[]{:T(128)}, f32[512,8,128]{0,2,1:T(8,128)}, ...), condition=%wide.region_9.10_spmd.clone, body=%wide.region_6.9_spmd.clone.sunk | while | flops 1083460608 | bytes 12099821 | solution.py:101
  177.9 4.0 bitcast_add_fusion.2
  185.4 5.6 bitcast_add_fusion.2
  194.3 5.6 bitcast_add_fusion.2
  203.2 5.6 bitcast_add_fusion.2
  213.0 42.4 %all-gather.15.cloned.1.call-done = bf16[2048,1024]{1,0:T(8,128)(2,1)} async-done(((bf16[512,1024]{1,0:T(8,128)(2,1)}), bf16[2048,1024]{1,0:T(8,128)(2,1)}) %all-gather.15.cloned.1.call-update) | async-done | bytes 4194320 | tf_op jit(solution)/shard_map/all_gather | solution.py:105
  255.5 6.4 copy.65
  261.9 15.2 %all_gather.25 = f32[2048,8]{0,1:T(8,128)S(1)} all-gather(f32[512,8]{0,1:T(8,128)S(1)} %bitcast.132), channel_id=1, replica_groups=mesh['heads'=4,'tokens'=4,'cols'=2] {'tokens'}, dimensions={0}, use_global_device_ids=true | all-gather | bytes 81920 | tf_op jit(solution)/shard_map/all_gather | solution.py:103
  277.1 59.8 %all-gather.13.cloned.1.call-done = bf16[2048,1024]{0,1:T(8,128)(2,1)} async-done(((bf16[512,1024]{0,1:T(8,128)(2,1)}), bf16[2048,1024]{0,1:T(8,128)(2,1)}) %all-gather.13.cloned.1.call-update) | async-done | bytes 4194320 | tf_op jit(solution)/shard_map/all_gather | solution.py:104
  336.9 14.4 %fusion.29 = bf16[8,512,128]{1,2,0:T(8,128)(2,1)S(1)} fusion(bf16[2048,8,128]{0,2,1:T(8,128)(2,1)} %bitcast.130, bf16[2048,8,128]{0,2,1:T(8,128)(2,1)} %bitcast.134, f32[8,2048]{1,0:T(8,128)S(1)} %bitcast.133, pred[2048,512]{1,0:T(8,128)(4,1)S(1)} %broadcast_compare_fusion.2, bf16[512,1024]{1,0:T(8,128)(2,1)S(1)} %copy-done.2), kind=kOutput, calls=%fused_computation.50 | convolution fusion | flops 4329046016 | bytes 11599872 | tf_op jit(solution)/shard_map/hqk,qhd->khd/dot_general | solution.py:115
  353.0 109.4 %all-gather.11.cloned.1.call-done = bf16[8,512,1024]{2,1,0:T(8,128)(2,1)} async-done(((bf16[1,512,1024]{2,1,0:T(8,128)(2,1)}), bf16[8,512,1024]{2,1,0:T(8,128)(2,1)}) %all-gather.11.cloned.1.call-update) | async-done | bytes 8388624 | tf_op jit(solution)/shard_map/all_gather | solution.py:122
  462.4 4.5 fusion.27
  466.9 120.8 %all-gather.17.cloned.1.call-done = bf16[8,512,1024]{2,1,0:T(8,128)(2,1)} async-done(((bf16[1,512,1024]{2,1,0:T(8,128)(2,1)}), bf16[8,512,1024]{2,1,0:T(8,128)(2,1)}) %all-gather.17.cloned.1.call-update) | async-done | bytes 8388624 | tf_op jit(solution)/shard_map/all_gather | solution.py:123
  587.6 4.4 fusion.26
  592.1 11.5 %copy.60 = bf16[2,1024,4,512]{3,1,0,2:T(8,128)(2,1)} copy(bf16[2,1024,4,512]{1,3,0,2:T(8,128)(2,1)} %bitcast.124) | data formatting | bytes 16777216 | tf_op jit(solution)/shard_map/acnf,ang->cfg/dot_general | solution.py:135
  603.6 11.5 %copy.67 = bf16[2,1024,4,512]{3,1,0,2:T(8,128)(2,1)} copy(bf16[2,1024,4,512]{1,3,0,2:T(8,128)(2,1)} %bitcast.126) | data formatting | bytes 16777216 | tf_op jit(solution)/shard_map/acnf,ang->cfg/dot_general | solution.py:138
  615.1 128.2 %all-reduce.3.cloned.1.call-done = (bf16[4,512,1024]{2,1,0:T(8,128)(2,1)}, bf16[4,512,1024]{2,1,0:T(8,128)(2,1)}) async-done(((bf16[4,512,1024]{2,1,0:T(8,128)(2,1)}, bf16[4,512,1024]{2,1,0:T(8,128)(2,1)}), (bf16[4,512,1024]{2,1,0:T(8,128)(2,1)}, bf16[4,512,1024]{2,1,0:T(8,128)(2,1)})) %all-reduce.3.cloned.1.call-update) | async-done | bytes 8388624 | tf_op jit(solution)/shard_map/psum | solution.py:13
  743.3 14.6 %bitcast_multiply_fusion.1 = f32[2048,1024]{1,0:T(8,128)} fusion(bf16[2048,4,512]{2,0,1:T(8,128)(2,1)} %bitcast.128, bf16[4,512,1024]{2,1,0:T(8,128)(2,1)} %get-tuple-element.383), kind=kOutput, calls=%fused_computation.43 | convolution fusion | flops 8592031744 | bytes 20971520 | tf_op jit(solution)/shard_map/acnf,ang->cfg/dot_general | solution.py:135
  757.9 11.0 %bitcast_multiply_fusion = f32[2048,1024]{1,0:T(8,128)} fusion(bf16[2048,4,512]{2,0,1:T(8,128)(2,1)S(1)} %bitcast.127, bf16[4,512,1024]{2,1,0:T(8,128)(2,1)S(1)} %copy-done.4), kind=kOutput, calls=%fused_computation.42 | convolution fusion | flops 8592031744 | bytes 20971520 | tf_op jit(solution)/shard_map/acnf,ang->cfg/dot_general | solution.py:138
  (116 shorter events, 43.7 us)
Async XLA Ops:
  7.2 86.1 %copy-start = (bf16[512,1024]{1,0:T(8,128)(2,1)S(1)}, bf16[512,1024]{1,0:T(8,128)(2,1)}, u32[]{:S(2)}) copy-start(bf16[512,1024]{1,0:T(8,128)(2,1)} %param.9) | copy-start | bytes 3145732
  7.2 86.1 %copy-start.3 = (s32[6]{0:T(128)S(1)}, s32[6]{0:T(128)}, u32[]{:S(2)}) copy-start(s32[6]{0:T(128)} %param.13) | copy-start | bytes 76
  7.2 86.0 %all-gather.9.cloned.1.call-start = ((), (), s32[]{:S(2)}) async-start(), calls=%async_computation.1 | async-start | bytes 5242880 | tf_op jit(solution)/shard_map/all_gather | solution.py:39
  9.6 165.0 %all-gather.7.cloned.1.call-start = ((), (), s32[]{:S(2)}) async-start(), calls=%async_computation | async-start | bytes 5242880 | tf_op jit(solution)/shard_map/all_gather | solution.py:40
  12.0 243.5 %all-gather.15.cloned.1.call-start = ((), (), s32[]{:S(2)}) async-start(), calls=%async_computation.4 | async-start | bytes 5242880 | tf_op jit(solution)/shard_map/all_gather | solution.py:105
  12.7 324.2 %all-gather.13.cloned.1.call-start = ((), (), s32[]{:S(2)}) async-start(), calls=%async_computation.3 | async-start | bytes 5242880 | tf_op jit(solution)/shard_map/all_gather | solution.py:104
  15.0 447.3 %all-gather.11.cloned.1.call-start = ((), (), s32[]{:S(2)}) async-start(), calls=%async_computation.2 | async-start | bytes 9437184 | tf_op jit(solution)/shard_map/all_gather | solution.py:122
  208.8 128.1 %copy-start.2 = (bf16[512,1024]{1,0:T(8,128)(2,1)S(1)}, bf16[512,1024]{1,0:T(8,128)(2,1)}, u32[]{:S(2)}) copy-start(bf16[512,1024]{1,0:T(8,128)(2,1)} %param.10) | copy-start | bytes 3145732
  212.0 375.6 %all-gather.17.cloned.1.call-start = ((), (), s32[]{:S(2)}) async-start(), calls=%async_computation.5 | async-start | bytes 9437184 | tf_op jit(solution)/shard_map/all_gather | solution.py:123
  352.7 390.6 %all-reduce.3.cloned.1.call-start = ((), (), s32[]{:S(2)}) async-start(), calls=%async_computation.6 | async-start | bytes 16777216 | tf_op jit(solution)/shard_map/psum | solution.py:13
  743.3 14.6 %copy-start.1 = (bf16[2,1024,4,512]{3,1,0,2:T(8,128)(2,1)S(1)}, bf16[2,1024,4,512]{3,1,0,2:T(8,128)(2,1)}, u32[]{:S(2)}) copy-start(bf16[2,1024,4,512]{3,1,0,2:T(8,128)(2,1)} %copy.67) | copy-start | bytes 25165828
  743.3 14.6 %copy-start.4 = (bf16[4,512,1024]{2,1,0:T(8,128)(2,1)S(1)}, bf16[4,512,1024]{2,1,0:T(8,128)(2,1)}, u32[]{:S(2)}) copy-start(bf16[4,512,1024]{2,1,0:T(8,128)(2,1)} %get-tuple-element.384) | copy-start | bytes 12582916
Sparse Core Ops, SparseCore 0:
  9.7 83.4 all-gather.8
  95.4 79.2 all-gather.6
  176.2 79.2 all-gather.14
  256.9 79.9 all-gather.12
  339.5 122.8 all-gather.10
  464.9 122.6 all-gather.16
  592.2 151.0 all-reduce.2
where the time goes:
time: 777 us; the launch traced here: 776 us
  waiting for transfers between devices  594 us (76%)
  matrix products  67.8 us (9%)
  local copies, waits for them, and re-layouts  56 us (7%)
  other arithmetic  22.4 us (3%)
  blocking collectives  15.2 us (2%)
  between operations  14.2 us (2%)
    psum x1, waiting for transfers between devices, spread(): return lax.psum(kept, axis)  128 us
    all_gather x1, waiting for transfers between devices, on_device(): lax.all_gather(value_grads[None], ('tokens', 'cols'), axis=0, tiled=True)  121 us
    all_gather x1, waiting for transfers between devices, on_device(): lax.all_gather(attended[None], ('tokens', 'cols'), axis=0, tiled=True)  109 us
    all_gather x1, waiting for transfers between devices, on_device(): lax.all_gather(key_in, 'tokens', axis=0, tiled=True)  78.1 us
    all_gather x1, waiting for transfers between devices, on_device(): query_rows = lax.all_gather(query_in, 'tokens', axis=0, tiled=True)  59.8 us
    all_gather x1, waiting for transfers between devices, on_device(): lax.all_gather(value_in, 'tokens', axis=0, tiled=True)  54.3 us
    all_gather x1, waiting for transfers between devices, on_device(): grad_rows = lax.all_gather(out_grads, 'tokens', axis=0, tiled=True)  42.4 us
    dot_general x4, matrix products, update(): jnp.einsum('hqk,khd->qhd', weights, value_rows, preferred_element_type=jn...  20.8 us
  transfers between devices with their start and end apart: 7, of which 7 were waited for; matrix products, arithmetic and copies ran while one was open for 15% of the time, Pallas kernels for 0%

commit v1 on v0

--- a/solution.py
+++ b/solution.py
@@ -102,7 +102,14 @@
     attended = weighted.reshape(tok_dev, row_width).astype(jnp.bfloat16)
     stats_all = lax.all_gather(log_total.T, "tokens", axis=0, tiled=True)
     query_rows = lax.all_gather(query_in, "tokens", axis=0, tiled=True)
-    grad_rows = lax.all_gather(out_grads, "tokens", axis=0, tiled=True)
+    ring = [out_grads]
+    for hop in range(3):
+        ring.append(lax.ppermute(ring[-1], "tokens", [(dev, (dev + 1) % 4) for dev in range(4)]))
+    grad_rows = jnp.roll(
+        jnp.concatenate(ring[::-1], axis=0),
+        (lax.axis_index("tokens") + 1) * ring[0].shape[0],
+        axis=0,
+    )
     piece_rows = query_rows.shape[0]
     piece_pos = jnp.arange(piece_rows, dtype=jnp.int32)
 

time: 777 us -> 745 us (0.959)
  waiting for transfers between devices: 594 us -> 486 us
  starting transfers between devices: 0.51 us -> 28.5 us
  blocking collectives: 15.2 us -> 32.6 us
  matrix products: 67.8 us -> 81.8 us
  other arithmetic: 22.4 us -> 33 us
    ppermute x0 -> x3, waiting for transfers between devices: none -> 123 us  [on_device(): lax.ppermute(ring[-1], 'tokens', [(dev, (dev + 1) % 4) for dev in range(4)])]
    all_gather x1, waiting for transfers between devices: 78.1 us -> 0.01 us  [on_device(): lax.all_gather(key_in, 'tokens', axis=0, tiled=True)]
    all_gather x1, waiting for transfers between devices: 59.8 us -> 0.01 us  [on_device(): query_rows = lax.all_gather(query_in, 'tokens', axis=0, tiled=True)]
    all_gather x1 -> x0, waiting for transfers between devices: 42.4 us -> none  [on_device(): grad_rows = lax.all_gather(out_grads, 'tokens', axis=0, tiled=True)]
    all_gather x1, waiting for transfers between devices: 121 us -> 87.9 us  [on_device(): lax.all_gather(value_grads[None], ('tokens', 'cols'), axis=0, tiled=True)]
    ppermute x0 -> x3, starting transfers between devices: none -> 28 us  [on_device(): lax.ppermute(ring[-1], 'tokens', [(dev, (dev + 1) % 4) for dev in range(4)])]
    all_gather x1, waiting for transfers between devices: 54.3 us -> 26.7 us  [on_device(): lax.all_gather(value_in, 'tokens', axis=0, tiled=True)]
    all_gather x1, blocking collectives: 15.2 us -> 32.6 us  [on_device(): stats_all = lax.all_gather(log_total.T, 'tokens', axis=0, tiled=True)]
  transfers between devices with their start and end apart: 7 -> 9, of which waited for: 7 -> 7; matrix products, arithmetic and copies ran while one was open for 15% -> 19% of each run, Pallas kernels for 0% -> 0%
where the time goes in v1:
time: 745 us; the launch traced here: 744 us
  waiting for transfers between devices  486 us (65%)
  matrix products  81.8 us (11%)
  local copies, waits for them, and re-layouts  61.6 us (8%)
  other arithmetic  33 us (4%)
  blocking collectives  32.6 us (4%)
  starting transfers between devices  28.5 us (4%)
  between operations  14.3 us (2%)
    psum x1, waiting for transfers between devices, spread(): return lax.psum(kept, axis)  128 us
    ppermute x3, waiting for transfers between devices, on_device(): lax.ppermute(ring[-1], 'tokens', [(dev, (dev + 1) % 4) for dev in range(4)])  123 us
    all_gather x1, waiting for transfers between devices, on_device(): lax.all_gather(attended[None], ('tokens', 'cols'), axis=0, tiled=True)  121 us
    all_gather x1, waiting for transfers between devices, on_device(): lax.all_gather(value_grads[None], ('tokens', 'cols'), axis=0, tiled=True)  87.9 us
    all_gather x1, blocking collectives, on_device(): stats_all = lax.all_gather(log_total.T, 'tokens', axis=0, tiled=True)  32.6 us
    ppermute x3, starting transfers between devices, on_device(): lax.ppermute(ring[-1], 'tokens', [(dev, (dev + 1) % 4) for dev in range(4)])  28 us
    all_gather x1, waiting for transfers between devices, on_device(): lax.all_gather(value_in, 'tokens', axis=0, tiled=True)  26.7 us
    dot_general x4, matrix products, update(): jnp.einsum('hqk,khd->qhd', weights, value_rows, preferred_element_type=jn...  21 us
  transfers between devices with their start and end apart: 9, of which 7 were waited for; matrix products, arithmetic and copies ran while one was open for 19% of the time, Pallas kernels for 0%

profile of v1, /device:TPU:0, one launch (start us, length us, event | category | flops | bytes accessed | tf_op | source)
XLA Modules:
  0.0 743.8 jit_solution(13328307158469663013)
XLA Ops:
  15.1 41.5 %collective-permute-done = bf16[512,1024]{1,0:T(8,128)(2,1)S(1)} collective-permute-done((bf16[512,1024]{1,0:T(8,128)(2,1)}, bf16[512,1024]{1,0:T(8,128)(2,1)S(1)}, u32[]{:S(2)}, u32[]{:S(2)}) %collective-permute-start) | collective-permute-done | bytes 1048608 | tf_op jit(solution)/shard_map/ppermute | solution.py:107
  56.6 17.8 %collective-permute-start.1 = (bf16[512,1024]{1,0:T(8,128)(2,1)S(1)}, bf16[512,1024]{1,0:T(8,128)(2,1)S(1)}, u32[]{:S(2)}, u32[]{:S(2)}) collective-permute-start(bf16[512,1024]{1,0:T(8,128)(2,1)S(1)} %collective-permute-done), channel_id=1, source_target_pairs={{0,2},{2,4},{4,6},{6,0},{1,3},{3,5},{5,7},{7,1},{8,10},{10,12},{12... | collective-permute-start | bytes 3145736 | tf_op jit(solution)/shard_map/ppermute | solution.py:107
  76.9 45.2 %collective-permute-done.1 = bf16[512,1024]{1,0:T(8,128)(2,1)S(1)} collective-permute-done((bf16[512,1024]{1,0:T(8,128)(2,1)S(1)}, bf16[512,1024]{1,0:T(8,128)(2,1)S(1)}, u32[]{:S(2)}, u32[]{:S(2)}) %collective-permute-start.1) | collective-permute-done | bytes 1048608 | tf_op jit(solution)/shard_map/ppermute | solution.py:107
  122.1 7.1 collective-permute-start.2
  130.9 36.1 %collective-permute-done.2 = bf16[512,1024]{1,0:T(8,128)(2,1)} collective-permute-done((bf16[512,1024]{1,0:T(8,128)(2,1)S(1)}, bf16[512,1024]{1,0:T(8,128)(2,1)}, u32[]{:S(2)}, u32[]{:S(2)}) %collective-permute-start.2) | collective-permute-done | bytes 1048608 | tf_op jit(solution)/shard_map/ppermute | solution.py:107
  172.5 6.4 copy.62
  178.9 50.3 %while.30 = (s32[]{:T(128)}, f32[8,512]{1,0:T(8,128)S(1)}, f32[8,512]{1,0:T(8,128)S(1)}, s32[6]{0:T(128)S(1)}, s32[4]{0:T(128)S(1)}, /*index=5*/bf16[2048,1024]{...) while((s32[]{:T(128)}, f32[8,512]{1,0:T(8,128)S(1)}, ...), condition=%wide.region_5.6_spmd.clone, body=%wide.region_0.5_spmd.clone.sunk | while | flops 553950208 | bytes 21995740 | solution.py:75
  181.9 5.1 fusion.59
  207.1 5.1 fusion.59
  219.6 5.1 fusion.59
  229.3 32.6 %all_gather.22 = f32[2048,8]{0,1:T(8,128)S(1)} all-gather(f32[512,8]{0,1:T(8,128)S(1)} %bitcast.132), channel_id=1, replica_groups=mesh['heads'=4,'tokens'=4,'cols'=2] {'tokens'}, dimensions={0}, use_global_device_ids=true | all-gather | bytes 81920 | tf_op jit(solution)/shard_map/all_gather | solution.py:103
  261.9 14.7 %fusion.29 = bf16[8,128,512]{2,1,0:T(8,128)(2,1)S(1)} fusion(bf16[2048,8,128]{0,2,1:T(8,128)(2,1)} %bitcast.130, bf16[2048,8,128]{0,2,1:T(8,128)(2,1)} %bitcast.134, f32[8,2048]{1,0:T(8,128)S(1)} %bitcast.133, pred[2048,512]{1,0:T(8,128)(4,1)} %broadcast_compare_fusion.2, bf16[512,1024]{1,0:T(8,128)(2,1)S(1)} %copy-done.3), kind=kOutput, calls=%fused_computation.50 | convolution fusion | flops 4329046016 | bytes 11599872 | tf_op jit(solution)/shard_map/hqk,qhd->khd/dot_general | solution.py:122
  278.0 26.7 %all-gather.6.cloned.1.call-done = bf16[2048,1024]{0,1:T(8,128)(2,1)} async-done(((bf16[512,1024]{0,1:T(8,128)(2,1)}), bf16[2048,1024]{0,1:T(8,128)(2,1)}) %all-gather.6.cloned.1.call-update) | async-done | bytes 4194320 | tf_op jit(solution)/shard_map/all_gather | solution.py:40
  304.7 34.5 %while.31 = (s32[]{:T(128)}, f32[512,8,128]{0,2,1:T(8,128)}, s32[4]{0:T(128)S(1)}, bf16[2048,1024]{0,1:T(8,128)(2,1)}, s32[6]{0:T(128)S(1)}, /*index=5*/bf16[204...) while((s32[]{:T(128)}, f32[512,8,128]{0,2,1:T(8,128)}, ...), condition=%wide.region_9.10_spmd.clone, body=%wide.region_6.9_spmd.clone.sunk | while | flops 1083460608 | bytes 12099813 | solution.py:101
  315.6 5.7 bitcast_add_fusion.2
  324.6 5.6 bitcast_add_fusion.2
  333.5 5.6 bitcast_add_fusion.2
  342.5 87.9 %all-gather.14.cloned.1.call-done = bf16[8,512,1024]{2,1,0:T(8,128)(2,1)} async-done(((bf16[1,512,1024]{2,1,0:T(8,128)(2,1)}), bf16[8,512,1024]{2,1,0:T(8,128)(2,1)}) %all-gather.14.cloned.1.call-update) | async-done | bytes 8388624 | tf_op jit(solution)/shard_map/all_gather | solution.py:130
  434.9 120.7 %all-gather.10.cloned.1.call-done = bf16[8,512,1024]{2,1,0:T(8,128)(2,1)} async-done(((bf16[1,512,1024]{2,1,0:T(8,128)(2,1)}), bf16[8,512,1024]{2,1,0:T(8,128)(2,1)}) %all-gather.10.cloned.1.call-update) | async-done | bytes 8388624 | tf_op jit(solution)/shard_map/all_gather | solution.py:129
  560.1 11.6 %copy.67 = bf16[2,1024,4,512]{3,1,0,2:T(8,128)(2,1)} copy(bf16[2,1024,4,512]{1,3,0,2:T(8,128)(2,1)} %bitcast.124) | data formatting | bytes 16777216 | tf_op jit(solution)/shard_map/acnf,ang->cfg/dot_general | solution.py:145
  571.7 11.4 %copy.60 = bf16[2,1024,4,512]{3,1,0,2:T(8,128)(2,1)} copy(bf16[2,1024,4,512]{1,3,0,2:T(8,128)(2,1)} %bitcast.126) | data formatting | bytes 16777216 | tf_op jit(solution)/shard_map/acnf,ang->cfg/dot_general | solution.py:142
  583.1 128.2 %all-reduce.3.cloned.1.call-done = (bf16[4,512,1024]{2,1,0:T(8,128)(2,1)}, bf16[4,512,1024]{2,1,0:T(8,128)(2,1)}) async-done(((bf16[4,512,1024]{2,1,0:T(8,128)(2,1)}, bf16[4,512,1024]{2,1,0:T(8,128)(2,1)}), (bf16[4,512,1024]{2,1,0:T(8,128)(2,1)}, bf16[4,512,1024]{2,1,0:T(8,128)(2,1)})) %all-reduce.3.cloned.1.call-update) | async-done | bytes 8388624 | tf_op jit(solution)/shard_map/psum | solution.py:13
  711.4 14.6 %bitcast_multiply_fusion = f32[2048,1024]{1,0:T(8,128)} fusion(bf16[2048,4,512]{2,0,1:T(8,128)(2,1)} %bitcast.128, bf16[4,512,1024]{2,1,0:T(8,128)(2,1)} %get-tuple-element.384), kind=kOutput, calls=%fused_computation.42 | convolution fusion | flops 8592031744 | bytes 20971520 | tf_op jit(solution)/shard_map/acnf,ang->cfg/dot_general | solution.py:145
  726.0 11.0 %bitcast_multiply_fusion.1 = f32[2048,1024]{1,0:T(8,128)} fusion(bf16[2048,4,512]{2,0,1:T(8,128)(2,1)S(1)} %bitcast.127, bf16[4,512,1024]{2,1,0:T(8,128)(2,1)S(1)} %copy-done.5), kind=kOutput, calls=%fused_computation.43 | convolution fusion | flops 8592031744 | bytes 20971520 | tf_op jit(solution)/shard_map/acnf,ang->cfg/dot_general | solution.py:142
  (130 shorter events, 78.1 us)
Async XLA Ops:
  7.2 161.2 %copy-start.2 = (bf16[512,1024]{1,0:T(8,128)(2,1)S(1)}, bf16[512,1024]{1,0:T(8,128)(2,1)}, u32[]{:S(2)}) copy-start(bf16[512,1024]{1,0:T(8,128)(2,1)} %param.12) | copy-start | bytes 3145732
  7.2 69.7 %copy-start.4 = (s32[6]{0:T(128)S(1)}, s32[6]{0:T(128)}, u32[]{:S(2)}) copy-start(s32[6]{0:T(128)} %param.13) | copy-start | bytes 76
  7.2 171.7 %all-gather.8.cloned.1.call-start = ((), (), s32[]{:S(2)}) async-start(), calls=%async_computation.1 | async-start | bytes 5242880 | tf_op jit(solution)/shard_map/all_gather | solution.py:39
  9.6 252.3 %all-gather.12.cloned.1.call-start = ((), (), s32[]{:S(2)}) async-start(), calls=%async_computation.3 | async-start | bytes 5242880 | tf_op jit(solution)/shard_map/all_gather | solution.py:104
  12.0 292.7 %all-gather.6.cloned.1.call-start = ((), (), s32[]{:S(2)}) async-start(), calls=%async_computation | async-start | bytes 5242880 | tf_op jit(solution)/shard_map/all_gather | solution.py:40
  12.0 44.6 %collective-permute-start = (bf16[512,1024]{1,0:T(8,128)(2,1)}, bf16[512,1024]{1,0:T(8,128)(2,1)S(1)}, u32[]{:S(2)}, u32[]{:S(2)}) collective-permute-start(bf16[512,1024]{1,0:T(8,128)(2,1)} %param.12), channel_id=1, source_target_pairs={{0,2},{2,4},{4,6},{6,0},{1,3},{3,5},{5,7},{7,1},{8,10},{10,12},{12... | collective-permute-start | bytes 3145736 | tf_op jit(solution)/shard_map/ppermute | solution.py:107
  56.6 65.5 %collective-permute-start.1 = (bf16[512,1024]{1,0:T(8,128)(2,1)S(1)}, bf16[512,1024]{1,0:T(8,128)(2,1)S(1)}, u32[]{:S(2)}, u32[]{:S(2)}) collective-permute-start(bf16[512,1024]{1,0:T(8,128)(2,1)S(1)} %collective-permute-done), channel_id=1, source_target_pairs={{0,2},{2,4},{4,6},{6,0},{1,3},{3,5},{5,7},{7,1},{8,10},{10,12},{12... | collective-permute-start | bytes 3145736 | tf_op jit(solution)/shard_map/ppermute | solution.py:107
  76.8 353.6 %all-gather.14.cloned.1.call-start = ((), (), s32[]{:S(2)}) async-start(), calls=%async_computation.4 | async-start | bytes 9437184 | tf_op jit(solution)/shard_map/all_gather | solution.py:130
  122.1 44.8 %collective-permute-start.2 = (bf16[512,1024]{1,0:T(8,128)(2,1)S(1)}, bf16[512,1024]{1,0:T(8,128)(2,1)}, u32[]{:S(2)}, u32[]{:S(2)}) collective-permute-start(bf16[512,1024]{1,0:T(8,128)(2,1)S(1)} %collective-permute-done.1), channel_id=1, source_target_pairs={{0,2},{2,4},{4,6},{6,0},{1,3},{3,5},{5,7},{7,1},{8,10},{10,12},{12... | collective-permute-start | bytes 3145736 | tf_op jit(solution)/shard_map/ppermute | solution.py:107
  170.0 8.9 %copy-start = (bf16[512,1024]{1,0:T(8,128)(2,1)S(1)}, bf16[512,1024]{1,0:T(8,128)(2,1)}, u32[]{:S(2)}) copy-start(bf16[512,1024]{1,0:T(8,128)(2,1)} %param.9) | copy-start | bytes 3145732
  178.9 83.0 %copy-start.3 = (bf16[512,1024]{1,0:T(8,128)(2,1)S(1)}, bf16[512,1024]{1,0:T(8,128)(2,1)}, u32[]{:S(2)}) copy-start(bf16[512,1024]{1,0:T(8,128)(2,1)} %param.10) | copy-start | bytes 3145732
  277.9 277.7 %all-gather.10.cloned.1.call-start = ((), (), s32[]{:S(2)}) async-start(), calls=%async_computation.2 | async-start | bytes 9437184 | tf_op jit(solution)/shard_map/all_gather | solution.py:129
  342.3 369.1 %all-reduce.3.cloned.1.call-start = ((), (), s32[]{:S(2)}) async-start(), calls=%async_computation.5 | async-start | bytes 16777216 | tf_op jit(solution)/shard_map/psum | solution.py:13
  711.4 14.6 %copy-start.1 = (bf16[2,1024,4,512]{3,1,0,2:T(8,128)(2,1)S(1)}, bf16[2,1024,4,512]{3,1,0,2:T(8,128)(2,1)}, u32[]{:S(2)}) copy-start(bf16[2,1024,4,512]{3,1,0,2:T(8,128)(2,1)} %copy.60) | copy-start | bytes 25165828
  711.4 14.6 %copy-start.5 = (bf16[4,512,1024]{2,1,0:T(8,128)(2,1)S(1)}, bf16[4,512,1024]{2,1,0:T(8,128)(2,1)}, u32[]{:S(2)}) copy-start(bf16[4,512,1024]{2,1,0:T(8,128)(2,1)} %get-tuple-element.383) | copy-start | bytes 12582916
Sparse Core Ops, SparseCore 0:
  9.7 121.1 all-gather.7
  132.5 89.9 all-gather.11
  224.0 80.5 all-gather.5
  307.2 123.1 all-gather.13
  432.9 122.6 all-gather.9
  560.2 151.0 all-reduce.2
